TPU v7x, 32 devices: a whole 2x2x4 slice. The times are simulated.
32 devices in a mesh: rows: 8 (over z, x), probe: 4 (over y, core).
Axes of the slice: x: 2, y: 2, z: 4, core: 2. Of those that a mesh axis runs over, the one named last changes fastest.
Arguments:
- start_block: float32 [8, 32768], P('probe', 'rows'), may hold values from -6 to 6
- blocks: bfloat16 [1024, 128, 128], P('rows'), may hold values from 0 to 3, as said below
- block_rows: int32 [1024], P('rows'), may hold values from 0 to 31
- block_cols: int32 [1024], P('rows'), may hold values from 0 to 63
- counts: int32 [8], P('rows'), may hold values from 32 to 128, as said below
- boundary: int32 [2, 16384], P(None, 'rows'), may hold values from 0 to 4095, as said below
Outputs:
- basis: float32 [8, 32768], P('probe', 'rows')
- alpha_blocks: float32 [3, 8, 8], replicated
- beta_blocks: float32 [3, 8, 8], replicated
Inputs may be any that keep to these rules, and one draw needn't show every extreme that they name: `blocks`: nonnegative edge weights, most entries zero. `counts`: one or more partitions have all 128 slots live. `boundary`: the 2048 entries of one list for one partition are distinct rows of that partition.
All inputs are finite; a program needn't handle non-finite values.
Results may differ from a plain program's by a relative error of at most 0.00525.
Values may be sent and summed in bfloat16 or wider, within the bound.
No kernel may reach another device: no remote copies, remote signals or barrier semaphores. Data moves between devices by JAX's collectives and lax.ppermute only.
A program may use at most 64 MiB of HBM per device.

v0:
```python
import functools

import jax
import jax.numpy as jnp
from jax import lax
from jax.experimental import pallas as pl
from jax.experimental.pallas import tpu as pltpu
from jax.sharding import PartitionSpec as P

STEPS = 3
SHIFTS = (0.0, 1.0, 0.0)
UNROLL = 8
CHUNK = 16
F32 = jnp.float32
BF16 = jnp.bfloat16

SMEM = pl.BlockSpec(memory_space=pltpu.SMEM)
VMEM = pl.BlockSpec(memory_space=pltpu.VMEM)
ANY = pl.BlockSpec(memory_space=pl.ANY)


def dot(a, b, contract):
    return lax.dot_general(a, b, (contract, ((), ())), preferred_element_type=F32)


def exact_dot(a, b, contract):
    return lax.dot_general(
        a, b, (contract, ((), ())), precision=lax.Precision.HIGHEST, preferred_element_type=F32
    )


def tile_copy(blocks, tiles, sems, chunk):
    part = pl.ds(chunk * CHUNK, CHUNK)
    return pltpu.make_async_copy(blocks.at[part], tiles.at[part], sems.at[chunk])


def start_tiles(live, blocks, tiles, sems):
    for chunk in range(blocks.shape[0] // CHUNK):
        @pl.when(chunk * CHUNK < live)
        def _():
            tile_copy(blocks, tiles, sems, chunk).start()


def wait_tiles(live, blocks, tiles, sems):
    for chunk in range(blocks.shape[0] // CHUNK):
        @pl.when(chunk * CHUNK < live)
        def _():
            tile_copy(blocks, tiles, sems, chunk).wait()


def for_slots(slots, live, body):
    def group(index, carry):
        entries = []
        for lane in range(UNROLL):
            code = slots[index * UNROLL + lane]
            entries.append((code & 255, (code >> 8) & 255, code >> 16))
        body(entries)
        return carry

    lax.fori_loop(0, (live + UNROLL - 1) // UNROLL, group, 0)


def two_parts(values):
    high = values.astype(BF16).astype(F32)
    return jnp.concatenate([high, values - high], axis=0)


def add_products(entries, tiles, source, totals, forward):
    products = []
    for slot, row, col in entries:
        index = col if forward else row
        got = dot(source[index], tiles[slot], ((1,), (1,)) if forward else ((1,), (0,)))
        products.append(got[: got.shape[0] // 2] + got[got.shape[0] // 2 :])
    for (slot, row, col), got in zip(entries, products):
        index = row if forward else col
        totals[index] = totals[index] + got


def fill_one_hot(bound, table):
    width = table.shape[0]
    halo = bound.shape[1]
    for part in range(2):
        for begin in range(0, halo, width):
            low = bound[part : part + 1, begin : begin + width] & (width - 1)
            hit = lax.broadcasted_iota(jnp.int32, (width, width), 0) == low
            table[:, part * halo + begin : part * halo + begin + width] = jnp.where(
                hit, 1.0, 0.0
            ).astype(BF16)


def add_boundary(bound, table, spread, values):
    width = table.shape[0]
    shift = width.bit_length() - 1
    high_count = spread.shape[0] // 16
    high = jnp.concatenate([bound[0:1, :], bound[1:2, :]], axis=1) >> shift
    stacked = two_parts(values)
    for index in range(high_count):
        spread[16 * index : 16 * index + 16, :] = jnp.where(high == index, stacked, 0.0).astype(BF16)
    got = dot(spread[...], table[...], ((1,), (1,)))
    return [got[16 * i : 16 * i + 8] + got[16 * i + 8 : 16 * i + 16] for i in range(high_count)]


def pick_boundary(bound, table, source, out_low, out_up):
    width = table.shape[0]
    shift = width.bit_length() - 1
    halo = bound.shape[1]
    edge = source.shape[2]
    ratio = width // edge
    high_count = (source.shape[0] - 1) // ratio
    rows = jnp.concatenate(
        [
            jnp.concatenate([source[ratio * i + j] for j in range(ratio)], axis=1)
            for i in range(high_count)
        ],
        axis=0,
    )
    for part, out in enumerate((out_low, out_up)):
        for begin in range(0, halo, width):
            got = dot(rows, table[:, part * halo + begin : part * halo + begin + width], ((1,), (0,)))
            high = bound[part : part + 1, begin : begin + width] >> shift
            total = jnp.zeros((8, width), F32)
            for index in range(high_count):
                one = got[16 * index : 16 * index + 8] + got[16 * index + 8 : 16 * index + 16]
                total = total + jnp.where(high == index, one, 0.0)
            out[0:8, begin : begin + width] = total


def setup_kernel(counts, block_rows, block_cols, blocks, own, halo, sizes, low, up, tiles, sums, sems):
    live = counts[0]
    edge = blocks.shape[1]
    halo_blocks = low.shape[0]
    row_blocks = 2 * halo_blocks
    start_tiles(live, blocks, tiles, sems)
    sums[...] = jnp.zeros_like(sums)

    def place(slot, carry):
        own_count, halo_count = carry
        row = block_rows[slot]
        col = block_cols[slot]
        outside = (col >= row_blocks).astype(jnp.int32)
        code = slot | (row << 8) | ((col - row_blocks * outside) << 16)
        own[own_count] = code
        halo[halo_count] = code
        return own_count + 1 - outside, halo_count + outside

    own_count, halo_count = lax.fori_loop(0, live, place, (0, 0))
    empty = (row_blocks << 8) | (row_blocks << 16)
    for lane in range(UNROLL):
        own[own_count + lane] = empty
        halo[halo_count + lane] = empty
    sizes[0] = own_count
    sizes[1] = halo_count
    wait_tiles(live, blocks, tiles, sems)

    def add(entries):
        parts = [
            jnp.sum(tiles[slot].astype(F32).reshape(edge // 8, 8, edge), axis=0)
            for slot, row, col in entries
        ]
        for (slot, row, col), part in zip(entries, parts):
            sums[col] = sums[col] + part

    for_slots(halo, halo_count, add)
    for index in range(halo_blocks):
        low[index : index + 1, :] = jnp.sum(sums[index], axis=0, keepdims=True)
        up[index : index + 1, :] = jnp.sum(sums[halo_blocks + index], axis=0, keepdims=True)


def degree_kernel(counts, own, halo, sizes, blocks, degree, tiles, row_sums, col_sums, sems):
    live = counts[0]
    edge = blocks.shape[1]
    start_tiles(live, blocks, tiles, sems)
    row_sums[...] = jnp.zeros_like(row_sums)
    col_sums[...] = jnp.zeros_like(col_sums)
    ones = jnp.ones((16, edge), BF16)
    wait_tiles(live, blocks, tiles, sems)

    def add_rows(entries):
        parts = [dot(ones, tiles[slot], ((1,), (1,)))[0:8] for slot, row, col in entries]
        for (slot, row, col), part in zip(entries, parts):
            row_sums[row] = row_sums[row] + part

    def add_both(entries):
        parts = [
            jnp.sum(tiles[slot].astype(F32).reshape(edge // 8, 8, edge), axis=0)
            for slot, row, col in entries
        ]
        add_rows(entries)
        for (slot, row, col), part in zip(entries, parts):
            col_sums[col] = col_sums[col] + part

    for_slots(own, sizes[0], add_both)
    for_slots(halo, sizes[1], add_rows)
    for index in range(row_sums.shape[0] - 1):
        degree[:, index * edge : (index + 1) * edge] = (
            1.0 + row_sums[index] + jnp.sum(col_sums[index], axis=0, keepdims=True)
        )


def send_products(sizes, halo, tiles, bound, table, vector, scale, source, sums, out_low, out_up):
    edge = source.shape[2]
    row_blocks = source.shape[0] - 1
    half = row_blocks // 2
    for index in range(row_blocks):
        part = slice(index * edge, (index + 1) * edge)
        source[index] = two_parts(scale[:, part] * vector[:, part]).astype(BF16)
    source[row_blocks] = jnp.zeros_like(source[row_blocks])
    sums[...] = jnp.zeros_like(sums)
    for_slots(
        halo, sizes[1], lambda entries: add_products(entries, tiles, source, sums, False)
    )
    for index in range(half):
        part = slice(index * edge, (index + 1) * edge)
        out_low[8:16, part] = sums[index]
        out_up[8:16, part] = sums[half + index]
    pick_boundary(bound, table, source, out_low, out_up)


def first_kernel(
    counts, halo, sizes, place, blocks, bound, degree, got_low, got_up, *rest
):
    starts = rest[:-10]
    out_low, out_up, vector, scale, source, tiles, table, spread, sums, sems = rest[-10:]
    live = counts[0]
    edge = blocks.shape[1]
    start_tiles(live, blocks, tiles, sems)
    fill_one_hot(bound, table)
    each = starts[0].shape[0]
    for block in range(len(starts)):
        rows = starts[0][...]
        for other in range(1, len(starts)):
            rows = jnp.where(place[0] == (block ^ other), starts[other][...], rows)
        vector[block * each : (block + 1) * each, :] = rows
    received = jnp.concatenate(
        [got[i : i + 1, :] for got in (got_low, got_up) for i in range(got.shape[0])], axis=1
    )
    received = jnp.broadcast_to(received, (8, received.shape[1]))
    width = table.shape[0]
    for index, part in enumerate(add_boundary(bound, table, spread, received)):
        cols = slice(index * width, (index + 1) * width)
        total = degree[:, cols] + part
        root = lax.rsqrt(total)
        scale[:, cols] = root * (1.5 - 0.5 * total * root * root)
    wait_tiles(live, blocks, tiles, sems)
    send_products(sizes, halo, tiles, bound, table, vector, scale, source, sums, out_low, out_up)


def own_kernel(counts, own, sizes, blocks, source, image, tiles, sums, sems):
    live = counts[0]
    edge = blocks.shape[1]
    start_tiles(live, blocks, tiles, sems)
    sums[...] = jnp.zeros_like(sums)
    wait_tiles(live, blocks, tiles, sems)

    def add(entries):
        add_products(entries, tiles, source, sums, True)
        add_products(entries, tiles, source, sums, False)

    for_slots(own, sizes[0], add)
    for index in range(sums.shape[0] - 1):
        image[:, index * edge : (index + 1) * edge] = sums[index]


def next_vector(
    shift, live, halo, sizes, blocks, bound, previous, scale, image, got_low, got_up,
    vector, tiles, table, spread, sums, outside, sems,
):
    edge = blocks.shape[1]
    fill_one_hot(bound, table)
    halo_blocks = got_low.shape[1] // edge
    for index in range(halo_blocks):
        part = slice(index * edge, (index + 1) * edge)
        outside[index] = two_parts(got_low[0:8, part]).astype(BF16)
        outside[halo_blocks + index] = two_parts(got_up[0:8, part]).astype(BF16)
    outside[2 * halo_blocks] = jnp.zeros_like(outside[0])
    received = jnp.concatenate([got_low[8:16, :], got_up[8:16, :]], axis=1)
    added = add_boundary(bound, table, spread, received)
    width = table.shape[0]
    ratio = width // edge
    for index in range(sums.shape[0] - 1):
        part = slice((index % ratio) * edge, (index % ratio + 1) * edge)
        sums[index] = (
            added[index // ratio][:, part] + image[:, index * edge : (index + 1) * edge]
        )
    wait_tiles(live, blocks, tiles, sems)
    for_slots(
        halo, sizes[1], lambda entries: add_products(entries, tiles, outside, sums, True)
    )
    for index in range(sums.shape[0] - 1):
        part = slice(index * edge, (index + 1) * edge)
        old = previous[:, part]
        root = scale[:, part]
        vector[:, part] = root * (root * old) + root * sums[index] - shift * old


def middle_kernel(
    shift, counts, halo, sizes, blocks, bound, previous, scale, image, got_low, got_up,
    out_low, out_up, vector, source, tiles, table, spread, sums, outside, sems,
):
    live = counts[0]
    start_tiles(live, blocks, tiles, sems)
    next_vector(
        shift, live, halo, sizes, blocks, bound, previous, scale, image, got_low, got_up,
        vector, tiles, table, spread, sums, outside, sems,
    )
    send_products(sizes, halo, tiles, bound, table, vector, scale, source, sums, out_low, out_up)


def three_parts(values):
    high = values.astype(BF16)
    rest = values - high.astype(F32)
    middle = rest.astype(BF16)
    return [high, middle, (rest - middle.astype(F32)).astype(BF16)]


def last_kernel(
    shift, counts, halo, sizes, blocks, bound, scale, image, got_low, got_up, *rest
):
    vectors = rest[:STEPS]
    gram, vector, tiles, table, spread, sums, outside, sems = rest[STEPS:]
    live = counts[0]
    start_tiles(live, blocks, tiles, sems)
    next_vector(
        shift, live, halo, sizes, blocks, bound, vectors[-1], scale, image, got_low, got_up,
        vector, tiles, table, spread, sums, outside, sems,
    )
    basis = jnp.concatenate([one[...] for one in vectors] + [vector[...]], axis=0)
    size = basis.shape[0]
    parts = jnp.concatenate(three_parts(basis), axis=0)
    wide = dot(parts, parts, ((1,), (1,)))
    total = sum(
        wide[i * size : (i + 1) * size, j * size : (j + 1) * size]
        for i in reversed(range(3))
        for j in reversed(range(3))
    )
    packed = jnp.concatenate([total[8 * i : 8 * i + 8, :] for i in range(size // 8)], axis=1)
    for copy in range(gram.shape[0] // 8):
        gram[8 * copy : 8 * copy + 8, :] = packed


def final_kernel(node_total, place, grams, *rest):
    vectors = rest[: STEPS + 1]
    basis, alphas, betas = rest[STEPS + 1 :]
    size = 8 * (STEPS + 1)
    packed = grams[0:8, :]
    for copy in range(1, grams.shape[0] // 8):
        packed = packed + grams[8 * copy : 8 * copy + 8, :]
    packed = packed * (1.0 / node_total)
    gram = jnp.concatenate(
        [packed[:, i * size : (i + 1) * size] for i in range(STEPS + 1)], axis=0
    )
    row_ids = lax.broadcasted_iota(jnp.int32, (size, size), 0)
    col_ids = lax.broadcasted_iota(jnp.int32, (size, size), 1)
    unit = jnp.where(row_ids == col_ids, 1.0, 0.0)
    work = jnp.concatenate([gram, unit], axis=1)
    rows = lax.broadcasted_iota(jnp.int32, (size, 2 * size), 0)
    pivots = jnp.ones((size, 2 * size), F32)
    for k in range(size):
        pivot = jnp.broadcast_to(work[k : k + 1, k : k + 1], (1, 2 * size))
        line = work[k : k + 1, :]
        factor = jnp.broadcast_to(work[:, k : k + 1], (size, 2 * size))
        pivots = jnp.where(rows == k, pivot, pivots)
        work = work - jnp.where(rows > k, factor * (line / pivot), 0.0)
    work = work / jnp.sqrt(pivots)
    upper = jnp.where(row_ids <= col_ids, work[:, :size], 0.0)
    inverse = work[:, size:]
    own = jnp.where(row_ids // 8 == col_ids // 8, inverse, 0.0)
    moved = jnp.concatenate(
        [jnp.zeros((8, size), F32)]
        + [
            jnp.concatenate(
                [jnp.zeros((8, 8), F32), own[8 * i : 8 * i + 8, : size - 8]], axis=1
            )
            for i in range(STEPS)
        ],
        axis=0,
    )
    by_last = exact_dot(moved, upper, ((1,), (1,)))
    by_own = exact_dot(own, upper, ((1,), (1,)))
    small = unit[0:8, 0:8]

    def piece(table, i, j):
        return table[8 * i : 8 * i + 8, 8 * j : 8 * j + 8]

    for j in range(STEPS):
        beta = piece(by_last, j + 1, j + 1)
        alpha = (1.0 - SHIFTS[j]) * small - piece(by_last, j + 1, j)
        if j:
            alpha = alpha + exact_dot(piece(by_own, j, j - 1), piece(by_last, j, j), ((1,), (0,)))
        betas[j] = jnp.where(row_ids[0:8, 0:8] >= col_ids[0:8, 0:8], beta, 0.0)
        alphas[j] = alpha
    last = inverse[size - 8 :, :] * (-1.0) ** STEPS
    each = basis.shape[0]
    ids = lax.broadcasted_iota(jnp.int32, (8, size), 0)
    chosen = jnp.zeros((8, size), F32)
    for index in range(each):
        line = jnp.sum(jnp.where(ids == place[0] * each + index, last, 0.0), axis=0, keepdims=True)
        chosen = jnp.where(ids == index, line, chosen)
    total = exact_dot(chosen, jnp.concatenate([one[...] for one in vectors], axis=0), ((1,), (0,)))
    basis[...] = total[0:each]


def local(start_block, blocks, block_rows, block_cols, counts, boundary):
    each, rows_dev = start_block.shape
    slot_count, edge, _ = blocks.shape
    halo_width = boundary.shape[1]
    parts = lax.axis_size("rows")
    groups = lax.axis_size("probe")
    node_total = rows_dev * parts
    row_blocks = rows_dev // edge
    halo_blocks = halo_width // edge
    probes = each * groups
    width = 2 * edge
    shape = jax.ShapeDtypeStruct
    place = lax.axis_index("probe").astype(jnp.int32).reshape(1)

    forward = [(i, (i + 1) % parts) for i in range(parts)]
    backward = [(target, source) for source, target in forward]

    def exchange(to_low, to_up):
        from_up = lax.ppermute(to_low, "rows", backward)
        from_low = lax.ppermute(to_up, "rows", forward)
        return from_low, from_up

    tile_scratch = pltpu.VMEM(blocks.shape, BF16)
    sems = pltpu.SemaphoreType.DMA((slot_count // CHUNK,))
    sums = pltpu.VMEM((row_blocks + 1, 8, edge), F32)
    table = pltpu.VMEM((width, 2 * halo_width), BF16)
    spread = pltpu.VMEM((16 * (rows_dev // width), 2 * halo_width), BF16)
    source_shape = (row_blocks + 1, 16, edge)

    def call(body, in_specs, out_shape, out_specs, scratch, name):
        return pl.pallas_call(
            body,
            out_shape=out_shape,
            in_specs=in_specs,
            out_specs=out_specs,
            scratch_shapes=scratch,
            name=name,
            compiler_params=pltpu.CompilerParams(vmem_limit_bytes=40 << 20),
        )

    starts = [start_block]
    for other in range(1, groups):
        pairs = [(i, i ^ other) for i in range(groups)]
        starts.append(lax.ppermute(start_block, "probe", pairs))

    own, halo, sizes, low, up = call(
        setup_kernel,
        [SMEM, SMEM, SMEM, ANY],
        (
            shape((slot_count + UNROLL,), jnp.int32),
            shape((slot_count + UNROLL,), jnp.int32),
            shape((2,), jnp.int32),
            shape((halo_blocks, edge), F32),
            shape((halo_blocks, edge), F32),
        ),
        (SMEM, SMEM, SMEM, VMEM, VMEM),
        [tile_scratch, sums, sems],
        "setup",
    )(counts, block_rows, block_cols, blocks)
    got_low, got_up = exchange(low, up)
    degree = call(
        degree_kernel,
        [SMEM, SMEM, SMEM, SMEM, ANY],
        shape((8, rows_dev), F32),
        VMEM,
        [tile_scratch, sums, sums, sems],
        "degree",
    )(counts, own, halo, sizes, blocks)

    message = shape((16, halo_width), F32)
    vector_shape = shape((probes, rows_dev), F32)
    to_low, to_up, vector, scale, source = call(
        first_kernel,
        [SMEM, SMEM, SMEM, SMEM, ANY] + [VMEM] * (4 + groups),
        (message, message, vector_shape, vector_shape, shape(source_shape, BF16)),
        (VMEM,) * 5,
        [tile_scratch, table, spread, sums, sems],
        "first",
    )(counts, halo, sizes, place, blocks, boundary, degree, got_low, got_up, *starts)

    vectors = [vector]
    for step in range(STEPS):
        got_low, got_up = exchange(to_low, to_up)
        image = call(
            own_kernel,
            [SMEM, SMEM, SMEM, ANY, VMEM],
            vector_shape,
            VMEM,
            [tile_scratch, sums, sems],
            f"own{step}",
        )(counts, own, sizes, blocks, source)
        scratch = [
            tile_scratch, table, spread, sums, pltpu.VMEM((2 * halo_blocks + 1, 16, edge), BF16), sems,
        ]
        if step + 1 < STEPS:
            to_low, to_up, vector, source = call(
                functools.partial(middle_kernel, SHIFTS[step]),
                [SMEM, SMEM, SMEM, ANY] + [VMEM] * 6,
                (message, message, vector_shape, shape(source_shape, BF16)),
                (VMEM,) * 4,
                scratch,
                f"middle{step}",
            )(counts, halo, sizes, blocks, boundary, vectors[-1], scale, image, got_low, got_up)
        else:
            grams, vector = call(
                functools.partial(last_kernel, SHIFTS[step]),
                [SMEM, SMEM, SMEM, ANY] + [VMEM] * (5 + STEPS),
                (shape((8 * parts, 128), F32), vector_shape),
                (VMEM,) * 2,
                scratch,
                "last",
            )(counts, halo, sizes, blocks, boundary, scale, image, got_low, got_up, *vectors)
        vectors.append(vector)
    gathered = lax.all_to_all(grams, "rows", 0, 0, tiled=True)
    return call(
        functools.partial(final_kernel, float(node_total)),
        [SMEM] + [VMEM] * (2 + STEPS),
        (
            shape((each, rows_dev), F32),
            shape((STEPS, probes, probes), F32),
            shape((STEPS, probes, probes), F32),
        ),
        (VMEM,) * 3,
        [],
        "final",
    )(place, gathered, *vectors)


def solution(mesh):
    in_specs = (
        P("probe", "rows"),
        P("rows", None, None),
        P("rows"),
        P("rows"),
        P("rows"),
        P(None, "rows"),
    )
    out_specs = (P("probe", "rows"), P(), P())
    return jax.shard_map(local, mesh=mesh, in_specs=in_specs, out_specs=out_specs, check_vma=False)
```

profile of v0, /device:TPU:0, one launch (start us, length us, event | category | flops | bytes accessed | tf_op | source)
XLA Modules:
  0.0 83.8 jit_solution(12086107914408966185)
XLA Ops:
  0.6 3.1 %collective-permute-start.3 = (f32[2,4096]{1,0:T(2,128)}, f32[2,4096]{1,0:T(2,128)S(1)}, u32[]{:S(2)}, u32[]{:S(2)}) collective-permute-start(f32[2,4096]{1,0:T(2,128)} %rest_0_.1), channel_id=1, source_target_pairs={{0,2},{1,3},{2,0},{3,1},{4,6},{5,7},{6,4},{7,5},{8,10},{9,11},{10,... | collective-permute-start | bytes 98312 | tf_op jit(solution)/shard_map/ppermute | solution.py:446
  3.7 0.0 collective-permute-start.2
  3.7 0.2 collective-permute-start.4
  4.5 0.0 copy-start
  4.5 2.2 %copy-done = bf16[128,128,128]{2,1,0:T(8,128)(2,1)S(1)} copy-done((bf16[128,128,128]{2,1,0:T(8,128)(2,1)S(1)}, bf16[128,128,128]{2,1,0:T(8,128)(2,1)}, u32[]{:S(2)}) %copy-start) | copy-done | bytes 4194328
  6.7 0.0 copy-start.4
  6.7 0.7 copy-done.4
  7.4 0.0 copy-start.5
  7.4 0.7 copy-done.5
  8.0 0.0 copy-start.2
  8.0 0.0 copy-start.3
  8.0 1.9 %setup.1 = (s32[136]{0:T(256)S(1)}, s32[136]{0:T(256)S(1)}, s32[2]{0:T(128)S(1)}, f32[16,128]{1,0:T(8,128)S(1)}, f32[16,128]{1,0:T(8,128)S(1)}) custom-call(s32[1]{0:T(128)S(6)} %copy.9.counts, s32[128]{0:T(128)S(1)} %copy-done.4, s32[128]{0:T(128)S(1)} %copy-done.5, bf16[128,128,128]{2,1,0:T(8,128)(2,1)S(1)} %copy-done), custom_call_target="tpu_custom_call" | custom-call | tf_op jit(solution)/shard_map/setup/pallas_call | solution.py:448
  9.9 2.0 %collective-permute-start = (f32[16,128]{1,0:T(8,128)S(1)}, f32[16,128]{1,0:T(8,128)S(1)}, u32[]{:S(2)}, u32[]{:S(2)}) collective-permute-start(f32[16,128]{1,0:T(8,128)S(1)} %get-tuple-element.26), channel_id=1, source_target_pairs={{0,4},{4,8},{8,12},{12,16},{16,20},{20,24},{24,28},{28,0},{1,5},{5... | collective-permute-start | bytes 24584 | tf_op jit(solution)/shard_map/ppermute | solution.py:422
  12.0 4.7 %collective-permute-start.1 = (f32[16,128]{1,0:T(8,128)S(1)}, f32[16,128]{1,0:T(8,128)S(1)}, u32[]{:S(2)}, u32[]{:S(2)}) collective-permute-start(f32[16,128]{1,0:T(8,128)S(1)} %get-tuple-element.27), channel_id=1, source_target_pairs={{4,0},{8,4},{12,8},{16,12},{20,16},{24,20},{28,24},{0,28},{5,1},{9... | collective-permute-start | bytes 24584 | tf_op jit(solution)/shard_map/ppermute | solution.py:421
  16.7 0.0 copy-start.1
  16.7 2.2 %copy-done.1 = bf16[128,128,128]{2,1,0:T(8,128)(2,1)S(1)} copy-done((bf16[128,128,128]{2,1,0:T(8,128)(2,1)S(1)}, bf16[128,128,128]{2,1,0:T(8,128)(2,1)}, u32[]{:S(2)}) %copy-start.1) | copy-done | bytes 4194328
  18.8 1.8 %degree.1 = f32[8,4096]{1,0:T(8,128)S(1)} custom-call(s32[1]{0:T(128)S(6)} %copy.9.counts, s32[136]{0:T(256)S(1)} %get-tuple-element.25.own, s32[136]{0:T(256)S(1)} %get-tuple-element.23.halo, s32[2]{0:T(128)S(1)} %get-tuple-element.24.sizes, bf16[128,128,128]{2,1,0:T(8,128)(2,1)S(1)} %copy-done.1), custom_call_target="tpu_custom_call" | custom-call | tf_op jit(solution)/shard_map/degree/pallas_call | solution.py:463
  20.7 0.0 collective-permute-done.got_low
  20.7 0.0 collective-permute-done.1.got_up
  20.7 0.0 collective-permute-done.3.rest_2_
  20.7 0.0 collective-permute-done.2.rest_1_
  20.7 0.0 collective-permute-done.4.rest_3_
  20.8 0.0 copy-done.2
  20.8 0.0 copy-done.3
  20.8 2.9 %first.1 = (f32[16,2048]{1,0:T(8,128)S(1)}, f32[16,2048]{1,0:T(8,128)S(1)}, f32[8,4096]{1,0:T(8,128)S(1)}, f32[8,4096]{1,0:T(8,128)S(1)}, bf16[33,16,128]{2,1,0:T(8,128)(2,1)S(1)}) custom-call(s32[1]{0:T(128)S(6)} %copy.9.counts, s32[136]{0:T(256)S(1)} %get-tuple-element.23.halo, s32[2]{0:T(128)S(1)} %get-tuple-element.24.sizes, s32[1]{0:T(128)} %bitcast.place, ...), custom_call_target="tpu_custom_call" | custom-call | tf_op jit(solution)/shard_map/first/pallas_call | solution.py:474
  23.7 0.1 collective-permute-start.5
  23.7 7.1 %collective-permute-start.6 = (f32[16,2048]{1,0:T(8,128)S(1)}, f32[16,2048]{1,0:T(8,128)S(1)}, u32[]{:S(2)}, u32[]{:S(2)}) collective-permute-start(f32[16,2048]{1,0:T(8,128)S(1)} %get-tuple-element.32), channel_id=1, source_target_pairs={{4,0},{8,4},{12,8},{16,12},{20,16},{24,20},{28,24},{0,28},{5,1},{9... | collective-permute-start | bytes 393224 | tf_op jit(solution)/shard_map/ppermute | solution.py:421
  30.8 1.4 %own0.1.image = f32[8,4096]{1,0:T(8,128)S(1)} custom-call(s32[1]{0:T(128)S(6)} %copy.9.counts, s32[136]{0:T(256)S(1)} %get-tuple-element.25.own, s32[2]{0:T(128)S(1)} %get-tuple-element.24.sizes, bf16[128,128,128]{2,1,0:T(8,128)(2,1)S(1)} %copy-done.1, bf16[33,16,128]{2,1,0:T(8,128)(2,1)S(1)} %get-tuple-element.30.source), custom_call_target="tpu_custom_call" | custom-call | tf_op jit(solution)/shard_map/own0/pallas_call | solution.py:486
  32.2 1.6 %collective-permute-done.5.got_low = f32[16,2048]{1,0:T(8,128)S(1)} collective-permute-done((f32[16,2048]{1,0:T(8,128)S(1)}, f32[16,2048]{1,0:T(8,128)S(1)}, u32[]{:S(2)}, u32[]{:S(2)}) %collective-permute-start.5) | collective-permute-done | bytes 131104 | tf_op jit(solution)/shard_map/ppermute | solution.py:422
  33.8 0.0 collective-permute-done.6.got_up
  33.8 3.3 %middle0.1 = (f32[16,2048]{1,0:T(8,128)S(1)}, f32[16,2048]{1,0:T(8,128)S(1)}, f32[8,4096]{1,0:T(8,128)S(1)}, bf16[33,16,128]{2,1,0:T(8,128)(2,1)S(1)}) custom-call(s32[1]{0:T(128)S(6)} %copy.9.counts, s32[136]{0:T(256)S(1)} %get-tuple-element.23.halo, s32[2]{0:T(128)S(1)} %get-tuple-element.24.sizes, bf16[128,128,128]{2,1,0:T(8,128)(2,1)S(1)} %copy-done.1, ...), custom_call_target="tpu_custom_call" | custom-call | tf_op jit(solution)/shard_map/middle0/pallas_call | solution.py:498
  37.2 0.1 collective-permute-start.7
  37.2 8.0 %collective-permute-start.8 = (f32[16,2048]{1,0:T(8,128)S(1)}, f32[16,2048]{1,0:T(8,128)S(1)}, u32[]{:S(2)}, u32[]{:S(2)}) collective-permute-start(f32[16,2048]{1,0:T(8,128)S(1)} %get-tuple-element.36), channel_id=1, source_target_pairs={{4,0},{8,4},{12,8},{16,12},{20,16},{24,20},{28,24},{0,28},{5,1},{9... | collective-permute-start | bytes 393224 | tf_op jit(solution)/shard_map/ppermute | solution.py:421
  45.3 1.4 %own1.1.image = f32[8,4096]{1,0:T(8,128)S(1)} custom-call(s32[1]{0:T(128)S(6)} %copy.9.counts, s32[136]{0:T(256)S(1)} %get-tuple-element.25.own, s32[2]{0:T(128)S(1)} %get-tuple-element.24.sizes, bf16[128,128,128]{2,1,0:T(8,128)(2,1)S(1)} %copy-done.1, bf16[33,16,128]{2,1,0:T(8,128)(2,1)S(1)} %get-tuple-element.34.source), custom_call_target="tpu_custom_call" | custom-call | tf_op jit(solution)/shard_map/own1/pallas_call | solution.py:486
  46.7 1.4 %collective-permute-done.7.got_low = f32[16,2048]{1,0:T(8,128)S(1)} collective-permute-done((f32[16,2048]{1,0:T(8,128)S(1)}, f32[16,2048]{1,0:T(8,128)S(1)}, u32[]{:S(2)}, u32[]{:S(2)}) %collective-permute-start.7) | collective-permute-done | bytes 131104 | tf_op jit(solution)/shard_map/ppermute | solution.py:422
  48.2 0.0 collective-permute-done.8.got_up
  48.2 3.3 %middle1.1 = (f32[16,2048]{1,0:T(8,128)S(1)}, f32[16,2048]{1,0:T(8,128)S(1)}, f32[8,4096]{1,0:T(8,128)S(1)}, bf16[33,16,128]{2,1,0:T(8,128)(2,1)S(1)}) custom-call(s32[1]{0:T(128)S(6)} %copy.9.counts, s32[136]{0:T(256)S(1)} %get-tuple-element.23.halo, s32[2]{0:T(128)S(1)} %get-tuple-element.24.sizes, bf16[128,128,128]{2,1,0:T(8,128)(2,1)S(1)} %copy-done.1, ...), custom_call_target="tpu_custom_call" | custom-call | tf_op jit(solution)/shard_map/middle1/pallas_call | solution.py:498
  51.5 0.1 collective-permute-start.9
  51.6 8.2 %collective-permute-start.10 = (f32[16,2048]{1,0:T(8,128)S(1)}, f32[16,2048]{1,0:T(8,128)S(1)}, u32[]{:S(2)}, u32[]{:S(2)}) collective-permute-start(f32[16,2048]{1,0:T(8,128)S(1)} %get-tuple-element.39), channel_id=1, source_target_pairs={{4,0},{8,4},{12,8},{16,12},{20,16},{24,20},{28,24},{0,28},{5,1},{9... | collective-permute-start | bytes 393224 | tf_op jit(solution)/shard_map/ppermute | solution.py:421
  59.8 1.4 %own2.1.image = f32[8,4096]{1,0:T(8,128)S(1)} custom-call(s32[1]{0:T(128)S(6)} %copy.9.counts, s32[136]{0:T(256)S(1)} %get-tuple-element.25.own, s32[2]{0:T(128)S(1)} %get-tuple-element.24.sizes, bf16[128,128,128]{2,1,0:T(8,128)(2,1)S(1)} %copy-done.1, bf16[33,16,128]{2,1,0:T(8,128)(2,1)S(1)} %get-tuple-element.37.source), custom_call_target="tpu_custom_call" | custom-call | tf_op jit(solution)/shard_map/own2/pallas_call | solution.py:486
  61.2 1.4 %collective-permute-done.9.got_low = f32[16,2048]{1,0:T(8,128)S(1)} collective-permute-done((f32[16,2048]{1,0:T(8,128)S(1)}, f32[16,2048]{1,0:T(8,128)S(1)}, u32[]{:S(2)}, u32[]{:S(2)}) %collective-permute-start.9) | collective-permute-done | bytes 131104 | tf_op jit(solution)/shard_map/ppermute | solution.py:422
  62.7 0.0 collective-permute-done.10.got_up
  62.7 2.6 %last.1 = (f32[64,128]{1,0:T(8,128)S(1)}, f32[8,4096]{1,0:T(8,128)S(1)}) custom-call(s32[1]{0:T(128)S(6)} %copy.9.counts, s32[136]{0:T(256)S(1)} %get-tuple-element.23.halo, s32[2]{0:T(128)S(1)} %get-tuple-element.24.sizes, bf16[128,128,128]{2,1,0:T(8,128)(2,1)S(1)} %copy-done.1, s32[2,2048]{1,0:T(2,128)S(1)} %copy-done.2, ...), custom_call_target="tpu_custom_call" | custom-call | tf_op jit(solution)/shard_map/last/pallas_call | solution.py:507
  65.2 14.5 %all_to_all.11 = f32[8,8,128]{2,1,0:T(8,128)S(1)} all-to-all(f32[8,8,128]{2,1,0:T(8,128)S(1)} %bitcast.4), channel_id=1, replica_groups=mesh['rows'=8,'probe'=4] {'rows'}, dimensions={0} | all-to-all | bytes 65536 | tf_op jit(solution)/shard_map/all_to_all | solution.py:516
  79.8 4.1 %final.1 = (f32[2,4096]{1,0:T(2,128)}, f32[3,8,8]{2,1,0:T(8,128)}, f32[3,8,8]{2,1,0:T(8,128)}) custom-call(s32[1]{0:T(128)} %bitcast.place, f32[64,128]{1,0:T(8,128)S(1)} %bitcast.3, f32[8,4096]{1,0:T(8,128)S(1)} %get-tuple-element.29.previous.rest_0_, f32[8,4096]{1,0:T(8,128)S(1)} %get-tuple-element.33.previous.rest_1_, ...), custom_call_target="tpu_custom_call" | custom-call | tf_op jit(solution)/shard_map/final/pallas_call | solution.py:517
Async XLA Ops:
  0.6 20.1 %collective-permute-start.3 = (f32[2,4096]{1,0:T(2,128)}, f32[2,4096]{1,0:T(2,128)S(1)}, u32[]{:S(2)}, u32[]{:S(2)}) collective-permute-start(f32[2,4096]{1,0:T(2,128)} %rest_0_.1), channel_id=1, source_target_pairs={{0,2},{1,3},{2,0},{3,1},{4,6},{5,7},{6,4},{7,5},{8,10},{9,11},{10,... | collective-permute-start | bytes 98312 | tf_op jit(solution)/shard_map/ppermute | solution.py:446
  3.7 17.0 %collective-permute-start.2 = (f32[2,4096]{1,0:T(2,128)}, f32[2,4096]{1,0:T(2,128)S(1)}, u32[]{:S(2)}, u32[]{:S(2)}) collective-permute-start(f32[2,4096]{1,0:T(2,128)} %rest_0_.1), channel_id=1, source_target_pairs={{0,1},{1,0},{2,3},{3,2},{4,5},{5,4},{6,7},{7,6},{8,9},{9,8},{10,11... | collective-permute-start | bytes 98312 | tf_op jit(solution)/shard_map/ppermute | solution.py:446
  3.7 17.0 %collective-permute-start.4 = (f32[2,4096]{1,0:T(2,128)}, f32[2,4096]{1,0:T(2,128)S(1)}, u32[]{:S(2)}, u32[]{:S(2)}) collective-permute-start(f32[2,4096]{1,0:T(2,128)} %rest_0_.1), channel_id=1, source_target_pairs={{0,3},{1,2},{2,1},{3,0},{4,7},{5,6},{6,5},{7,4},{8,11},{9,10},{10,... | collective-permute-start | bytes 98312 | tf_op jit(solution)/shard_map/ppermute | solution.py:446
  4.5 2.2 %copy-start = (bf16[128,128,128]{2,1,0:T(8,128)(2,1)S(1)}, bf16[128,128,128]{2,1,0:T(8,128)(2,1)}, u32[]{:S(2)}) copy-start(bf16[128,128,128]{2,1,0:T(8,128)(2,1)} %blocks.17) | copy-start | bytes 12582916
  6.7 0.7 copy-start.4
  7.4 0.7 copy-start.5
  8.0 12.7 %copy-start.2 = (s32[2,2048]{1,0:T(2,128)S(1)}, s32[2,2048]{1,0:T(2,128)}, u32[]{:S(2)}) copy-start(s32[2,2048]{1,0:T(2,128)} %bound.7) | copy-start | bytes 49156
  8.0 12.7 %copy-start.3 = (f32[2,4096]{1,0:T(2,128)S(1)}, f32[2,4096]{1,0:T(2,128)}, u32[]{:S(2)}) copy-start(f32[2,4096]{1,0:T(2,128)} %rest_0_.1) | copy-start | bytes 98308
  9.9 10.8 %collective-permute-start = (f32[16,128]{1,0:T(8,128)S(1)}, f32[16,128]{1,0:T(8,128)S(1)}, u32[]{:S(2)}, u32[]{:S(2)}) collective-permute-start(f32[16,128]{1,0:T(8,128)S(1)} %get-tuple-element.26), channel_id=1, source_target_pairs={{0,4},{4,8},{8,12},{12,16},{16,20},{20,24},{24,28},{28,0},{1,5},{5... | collective-permute-start | bytes 24584 | tf_op jit(solution)/shard_map/ppermute | solution.py:422
  12.0 8.8 %collective-permute-start.1 = (f32[16,128]{1,0:T(8,128)S(1)}, f32[16,128]{1,0:T(8,128)S(1)}, u32[]{:S(2)}, u32[]{:S(2)}) collective-permute-start(f32[16,128]{1,0:T(8,128)S(1)} %get-tuple-element.27), channel_id=1, source_target_pairs={{4,0},{8,4},{12,8},{16,12},{20,16},{24,20},{28,24},{0,28},{5,1},{9... | collective-permute-start | bytes 24584 | tf_op jit(solution)/shard_map/ppermute | solution.py:421
  16.7 2.2 %copy-start.1 = (bf16[128,128,128]{2,1,0:T(8,128)(2,1)S(1)}, bf16[128,128,128]{2,1,0:T(8,128)(2,1)}, u32[]{:S(2)}) copy-start(bf16[128,128,128]{2,1,0:T(8,128)(2,1)} %blocks.17) | copy-start | bytes 12582916
  23.7 10.2 %collective-permute-start.5 = (f32[16,2048]{1,0:T(8,128)S(1)}, f32[16,2048]{1,0:T(8,128)S(1)}, u32[]{:S(2)}, u32[]{:S(2)}) collective-permute-start(f32[16,2048]{1,0:T(8,128)S(1)} %get-tuple-element.31), channel_id=1, source_target_pairs={{0,4},{4,8},{8,12},{12,16},{16,20},{20,24},{24,28},{28,0},{1,5},{5... | collective-permute-start | bytes 393224 | tf_op jit(solution)/shard_map/ppermute | solution.py:422
  23.7 10.1 %collective-permute-start.6 = (f32[16,2048]{1,0:T(8,128)S(1)}, f32[16,2048]{1,0:T(8,128)S(1)}, u32[]{:S(2)}, u32[]{:S(2)}) collective-permute-start(f32[16,2048]{1,0:T(8,128)S(1)} %get-tuple-element.32), channel_id=1, source_target_pairs={{4,0},{8,4},{12,8},{16,12},{20,16},{24,20},{28,24},{0,28},{5,1},{9... | collective-permute-start | bytes 393224 | tf_op jit(solution)/shard_map/ppermute | solution.py:421
  37.2 11.0 %collective-permute-start.7 = (f32[16,2048]{1,0:T(8,128)S(1)}, f32[16,2048]{1,0:T(8,128)S(1)}, u32[]{:S(2)}, u32[]{:S(2)}) collective-permute-start(f32[16,2048]{1,0:T(8,128)S(1)} %get-tuple-element.35), channel_id=1, source_target_pairs={{0,4},{4,8},{8,12},{12,16},{16,20},{20,24},{24,28},{28,0},{1,5},{5... | collective-permute-start | bytes 393224 | tf_op jit(solution)/shard_map/ppermute | solution.py:422
  37.2 10.9 %collective-permute-start.8 = (f32[16,2048]{1,0:T(8,128)S(1)}, f32[16,2048]{1,0:T(8,128)S(1)}, u32[]{:S(2)}, u32[]{:S(2)}) collective-permute-start(f32[16,2048]{1,0:T(8,128)S(1)} %get-tuple-element.36), channel_id=1, source_target_pairs={{4,0},{8,4},{12,8},{16,12},{20,16},{24,20},{28,24},{0,28},{5,1},{9... | collective-permute-start | bytes 393224 | tf_op jit(solution)/shard_map/ppermute | solution.py:421
  51.5 11.2 %collective-permute-start.9 = (f32[16,2048]{1,0:T(8,128)S(1)}, f32[16,2048]{1,0:T(8,128)S(1)}, u32[]{:S(2)}, u32[]{:S(2)}) collective-permute-start(f32[16,2048]{1,0:T(8,128)S(1)} %get-tuple-element.38), channel_id=1, source_target_pairs={{0,4},{4,8},{8,12},{12,16},{16,20},{20,24},{24,28},{28,0},{1,5},{5... | collective-permute-start | bytes 393224 | tf_op jit(solution)/shard_map/ppermute | solution.py:422
  51.6 11.1 %collective-permute-start.10 = (f32[16,2048]{1,0:T(8,128)S(1)}, f32[16,2048]{1,0:T(8,128)S(1)}, u32[]{:S(2)}, u32[]{:S(2)}) collective-permute-start(f32[16,2048]{1,0:T(8,128)S(1)} %get-tuple-element.39), channel_id=1, source_target_pairs={{4,0},{8,4},{12,8},{16,12},{20,16},{24,20},{28,24},{0,28},{5,1},{9... | collective-permute-start | bytes 393224 | tf_op jit(solution)/shard_map/ppermute | solution.py:421
where the time goes:
time: 84.8 us; the launch traced here: 83.8 us
  starting transfers between devices  33.5 us (40%)
  Pallas kernels  24.1 us (28%)
  blocking collectives  14.5 us (17%)
  local copies, waits for them, and re-layouts  5.69 us (7%)
  waiting for transfers between devices  4.54 us (5%)
  between operations  1.45 us (2%)
    ppermute x4, starting transfers between devices, exchange(): from_up = lax.ppermute(to_low, 'rows', backward)  28 us
    all_to_all x1, blocking collectives, local(): gathered = lax.all_to_all(grams, 'rows', 0, 0, tiled=True)  14.5 us
    pallas_call x2, Pallas kernels, local(): call(functools.partial(middle_kernel, SHIFTS[step]), [SMEM, SMEM, SMEM, A...  6.66 us
    unnamed x12, local copies, waits for them, and re-layouts  5.69 us
    ppermute x4, waiting for transfers between devices, exchange(): from_low = lax.ppermute(to_up, 'rows', forward)  4.52 us
    pallas_call x3, Pallas kernels, local(): call(own_kernel, [SMEM, SMEM, SMEM, ANY, VMEM], vector_shape, VMEM, [tile...  4.27 us
    pallas_call x1, Pallas kernels, local(): call(functools.partial(final_kernel, float(node_total)), [SMEM] + [VMEM]...  4.05 us
    ppermute x3, starting transfers between devices, local(): starts.append(lax.ppermute(start_block, 'probe', pairs))  3.25 us
  transfers between devices with their start and end apart: 11, of which 3 were waited for; matrix products, arithmetic and copies ran while one was open for 0% of the time, Pallas kernels for 10%

commit v1 on v0

--- a/solution.py
+++ b/solution.py
@@ -10,7 +10,7 @@
 STEPS = 3
 SHIFTS = (0.0, 1.0, 0.0)
 UNROLL = 8
-CHUNK = 16
+LIMIT = 16 << 20
 F32 = jnp.float32
 BF16 = jnp.bfloat16
 
@@ -27,25 +27,6 @@
     return lax.dot_general(
         a, b, (contract, ((), ())), precision=lax.Precision.HIGHEST, preferred_element_type=F32
     )
-
-
-def tile_copy(blocks, tiles, sems, chunk):
-    part = pl.ds(chunk * CHUNK, CHUNK)
-    return pltpu.make_async_copy(blocks.at[part], tiles.at[part], sems.at[chunk])
-
-
-def start_tiles(live, blocks, tiles, sems):
-    for chunk in range(blocks.shape[0] // CHUNK):
-        @pl.when(chunk * CHUNK < live)
-        def _():
-            tile_copy(blocks, tiles, sems, chunk).start()
-
-
-def wait_tiles(live, blocks, tiles, sems):
-    for chunk in range(blocks.shape[0] // CHUNK):
-        @pl.when(chunk * CHUNK < live)
-        def _():
-            tile_copy(blocks, tiles, sems, chunk).wait()
 
 
 def for_slots(slots, live, body):
@@ -125,13 +106,18 @@
             out[0:8, begin : begin + width] = total
 
 
-def setup_kernel(counts, block_rows, block_cols, blocks, own, halo, sizes, low, up, tiles, sums, sems):
-    live = counts[0]
-    edge = blocks.shape[1]
-    halo_blocks = low.shape[0]
-    row_blocks = 2 * halo_blocks
-    start_tiles(live, blocks, tiles, sems)
-    sums[...] = jnp.zeros_like(sums)
+def list_kernel(
+    row_blocks, counts_in, rows_in, cols_in, own, halo, sizes, counts, block_rows, block_cols, sems
+):
+    pairs = ((counts_in, counts), (rows_in, block_rows), (cols_in, block_cols))
+    copies = [
+        pltpu.make_async_copy(source, target, sems.at[index])
+        for index, (source, target) in enumerate(pairs)
+    ]
+    for copy in copies:
+        copy.start()
+    for copy in copies:
+        copy.wait()
 
     def place(slot, carry):
         own_count, halo_count = carry
@@ -143,14 +129,19 @@
         halo[halo_count] = code
         return own_count + 1 - outside, halo_count + outside
 
-    own_count, halo_count = lax.fori_loop(0, live, place, (0, 0))
+    own_count, halo_count = lax.fori_loop(0, counts[0], place, (0, 0))
     empty = (row_blocks << 8) | (row_blocks << 16)
     for lane in range(UNROLL):
         own[own_count + lane] = empty
         halo[halo_count + lane] = empty
     sizes[0] = own_count
     sizes[1] = halo_count
-    wait_tiles(live, blocks, tiles, sems)
+
+
+def setup_kernel(halo, sizes, tiles, low, up, sums):
+    edge = tiles.shape[1]
+    halo_blocks = low.shape[0]
+    sums[...] = jnp.zeros_like(sums)
 
     def add(entries):
         parts = [
@@ -160,20 +151,18 @@
         for (slot, row, col), part in zip(entries, parts):
             sums[col] = sums[col] + part
 
-    for_slots(halo, halo_count, add)
+    for_slots(halo, sizes[1], add)
     for index in range(halo_blocks):
         low[index : index + 1, :] = jnp.sum(sums[index], axis=0, keepdims=True)
         up[index : index + 1, :] = jnp.sum(sums[halo_blocks + index], axis=0, keepdims=True)
 
 
-def degree_kernel(counts, own, halo, sizes, blocks, degree, tiles, row_sums, col_sums, sems):
-    live = counts[0]
-    edge = blocks.shape[1]
-    start_tiles(live, blocks, tiles, sems)
+def degree_kernel(own, halo, sizes, tiles, bound, degree, table, row_sums, col_sums):
+    edge = tiles.shape[1]
+    fill_one_hot(bound, table)
     row_sums[...] = jnp.zeros_like(row_sums)
     col_sums[...] = jnp.zeros_like(col_sums)
     ones = jnp.ones((16, edge), BF16)
-    wait_tiles(live, blocks, tiles, sems)
 
     def add_rows(entries):
         parts = [dot(ones, tiles[slot], ((1,), (1,)))[0:8] for slot, row, col in entries]
@@ -217,19 +206,16 @@
 
 
 def first_kernel(
-    counts, halo, sizes, place, blocks, bound, degree, got_low, got_up, *rest
+    halo, sizes, tiles, bound, table, degree, got_low, got_up, *rest
 ):
-    starts = rest[:-10]
-    out_low, out_up, vector, scale, source, tiles, table, spread, sums, sems = rest[-10:]
-    live = counts[0]
-    edge = blocks.shape[1]
-    start_tiles(live, blocks, tiles, sems)
-    fill_one_hot(bound, table)
+    starts = rest[:-7]
+    out_low, out_up, vector, scale, source, spread, sums = rest[-7:]
     each = starts[0].shape[0]
+    place = lax.axis_index("probe")
     for block in range(len(starts)):
         rows = starts[0][...]
         for other in range(1, len(starts)):
-            rows = jnp.where(place[0] == (block ^ other), starts[other][...], rows)
+            rows = jnp.where(place == (block ^ other), starts[other][...], rows)
         vector[block * each : (block + 1) * each, :] = rows
     received = jnp.concatenate(
         [got[i : i + 1, :] for got in (got_low, got_up) for i in range(got.shape[0])], axis=1
@@ -241,16 +227,12 @@
         total = degree[:, cols] + part
         root = lax.rsqrt(total)
         scale[:, cols] = root * (1.5 - 0.5 * total * root * root)
-    wait_tiles(live, blocks, tiles, sems)
     send_products(sizes, halo, tiles, bound, table, vector, scale, source, sums, out_low, out_up)
 
 
-def own_kernel(counts, own, sizes, blocks, source, image, tiles, sums, sems):
-    live = counts[0]
-    edge = blocks.shape[1]
-    start_tiles(live, blocks, tiles, sems)
+def own_kernel(own, sizes, tiles, source, image, sums):
+    edge = tiles.shape[1]
     sums[...] = jnp.zeros_like(sums)
-    wait_tiles(live, blocks, tiles, sems)
 
     def add(entries):
         add_products(entries, tiles, source, sums, True)
@@ -262,11 +244,10 @@
 
 
 def next_vector(
-    shift, live, halo, sizes, blocks, bound, previous, scale, image, got_low, got_up,
-    vector, tiles, table, spread, sums, outside, sems,
+    shift, halo, sizes, tiles, bound, table, previous, scale, image, got_low, got_up,
+    vector, spread, sums, outside,
 ):
-    edge = blocks.shape[1]
-    fill_one_hot(bound, table)
+    edge = tiles.shape[1]
     halo_blocks = got_low.shape[1] // edge
     for index in range(halo_blocks):
         part = slice(index * edge, (index + 1) * edge)
@@ -282,7 +263,6 @@
         sums[index] = (
             added[index // ratio][:, part] + image[:, index * edge : (index + 1) * edge]
         )
-    wait_tiles(live, blocks, tiles, sems)
     for_slots(
         halo, sizes[1], lambda entries: add_products(entries, tiles, outside, sums, True)
     )
@@ -294,14 +274,12 @@
 
 
 def middle_kernel(
-    shift, counts, halo, sizes, blocks, bound, previous, scale, image, got_low, got_up,
-    out_low, out_up, vector, source, tiles, table, spread, sums, outside, sems,
+    shift, halo, sizes, tiles, bound, table, previous, scale, image, got_low, got_up,
+    out_low, out_up, vector, source, spread, sums, outside,
 ):
-    live = counts[0]
-    start_tiles(live, blocks, tiles, sems)
     next_vector(
-        shift, live, halo, sizes, blocks, bound, previous, scale, image, got_low, got_up,
-        vector, tiles, table, spread, sums, outside, sems,
+        shift, halo, sizes, tiles, bound, table, previous, scale, image, got_low, got_up,
+        vector, spread, sums, outside,
     )
     send_products(sizes, halo, tiles, bound, table, vector, scale, source, sums, out_low, out_up)
 
@@ -314,15 +292,13 @@
 
 
 def last_kernel(
-    shift, counts, halo, sizes, blocks, bound, scale, image, got_low, got_up, *rest
+    shift, halo, sizes, tiles, bound, table, scale, image, got_low, got_up, *rest
 ):
     vectors = rest[:STEPS]
-    gram, vector, tiles, table, spread, sums, outside, sems = rest[STEPS:]
-    live = counts[0]
-    start_tiles(live, blocks, tiles, sems)
+    gram, vector, spread, sums, outside = rest[STEPS:]
     next_vector(
-        shift, live, halo, sizes, blocks, bound, vectors[-1], scale, image, got_low, got_up,
-        vector, tiles, table, spread, sums, outside, sems,
+        shift, halo, sizes, tiles, bound, table, vectors[-1], scale, image, got_low, got_up,
+        vector, spread, sums, outside,
     )
     basis = jnp.concatenate([one[...] for one in vectors] + [vector[...]], axis=0)
     size = basis.shape[0]
@@ -338,7 +314,7 @@
         gram[8 * copy : 8 * copy + 8, :] = packed
 
 
-def final_kernel(node_total, place, grams, *rest):
+def final_kernel(node_total, grams, *rest):
     vectors = rest[: STEPS + 1]
     basis, alphas, betas = rest[STEPS + 1 :]
     size = 8 * (STEPS + 1)
@@ -391,10 +367,11 @@
         alphas[j] = alpha
     last = inverse[size - 8 :, :] * (-1.0) ** STEPS
     each = basis.shape[0]
+    place = lax.axis_index("probe")
     ids = lax.broadcasted_iota(jnp.int32, (8, size), 0)
     chosen = jnp.zeros((8, size), F32)
     for index in range(each):
-        line = jnp.sum(jnp.where(ids == place[0] * each + index, last, 0.0), axis=0, keepdims=True)
+        line = jnp.sum(jnp.where(ids == place * each + index, last, 0.0), axis=0, keepdims=True)
         chosen = jnp.where(ids == index, line, chosen)
     total = exact_dot(chosen, jnp.concatenate([one[...] for one in vectors], axis=0), ((1,), (0,)))
     basis[...] = total[0:each]
@@ -412,7 +389,6 @@
     probes = each * groups
     width = 2 * edge
     shape = jax.ShapeDtypeStruct
-    place = lax.axis_index("probe").astype(jnp.int32).reshape(1)
 
     forward = [(i, (i + 1) % parts) for i in range(parts)]
     backward = [(target, source) for source, target in forward]
@@ -422,12 +398,9 @@
         from_low = lax.ppermute(to_up, "rows", forward)
         return from_low, from_up
 
-    tile_scratch = pltpu.VMEM(blocks.shape, BF16)
-    sems = pltpu.SemaphoreType.DMA((slot_count // CHUNK,))
     sums = pltpu.VMEM((row_blocks + 1, 8, edge), F32)
-    table = pltpu.VMEM((width, 2 * halo_width), BF16)
     spread = pltpu.VMEM((16 * (rows_dev // width), 2 * halo_width), BF16)
-    source_shape = (row_blocks + 1, 16, edge)
+    outside = pltpu.VMEM((2 * halo_blocks + 1, 16, edge), BF16)
 
     def call(body, in_specs, out_shape, out_specs, scratch, name):
         return pl.pallas_call(
@@ -437,7 +410,8 @@
             out_specs=out_specs,
             scratch_shapes=scratch,
             name=name,
-            compiler_params=pltpu.CompilerParams(vmem_limit_bytes=40 << 20),
+            compiler_params=pltpu.CompilerParams(vmem_limit_bytes=LIMIT),
+            cost_estimate=pl.CostEstimate(flops=2 << 30, transcendentals=0, bytes_accessed=1 << 20),
         )
 
     starts = [start_block]
@@ -445,78 +419,84 @@
         pairs = [(i, i ^ other) for i in range(groups)]
         starts.append(lax.ppermute(start_block, "probe", pairs))
 
-    own, halo, sizes, low, up = call(
+    listed = shape((slot_count + UNROLL,), jnp.int32)
+    own, halo, sizes = call(
+        functools.partial(list_kernel, row_blocks),
+        [ANY, ANY, ANY],
+        (listed, listed, shape((2,), jnp.int32)),
+        (SMEM, SMEM, SMEM),
+        [
+            pltpu.SMEM(counts.shape, jnp.int32),
+            pltpu.SMEM((slot_count,), jnp.int32),
+            pltpu.SMEM((slot_count,), jnp.int32),
+            pltpu.SemaphoreType.DMA((3,)),
+        ],
+        "lists",
+    )(counts, block_rows, block_cols)
+    low, up = call(
         setup_kernel,
-        [SMEM, SMEM, SMEM, ANY],
-        (
-            shape((slot_count + UNROLL,), jnp.int32),
-            shape((slot_count + UNROLL,), jnp.int32),
-            shape((2,), jnp.int32),
-            shape((halo_blocks, edge), F32),
-            shape((halo_blocks, edge), F32),
-        ),
-        (SMEM, SMEM, SMEM, VMEM, VMEM),
-        [tile_scratch, sums, sems],
+        [SMEM, SMEM, VMEM],
+        (shape((halo_blocks, edge), F32), shape((halo_blocks, edge), F32)),
+        (VMEM, VMEM),
+        [sums],
         "setup",
-    )(counts, block_rows, block_cols, blocks)
+    )(halo, sizes, blocks)
     got_low, got_up = exchange(low, up)
-    degree = call(
+    degree, table = call(
         degree_kernel,
-        [SMEM, SMEM, SMEM, SMEM, ANY],
-        shape((8, rows_dev), F32),
-        VMEM,
-        [tile_scratch, sums, sums, sems],
+        [SMEM, SMEM, SMEM, VMEM, VMEM],
+        (shape((8, rows_dev), F32), shape((width, 2 * halo_width), BF16)),
+        (VMEM, VMEM),
+        [sums, sums],
         "degree",
-    )(counts, own, halo, sizes, blocks)
+    )(own, halo, sizes, blocks, boundary)
 
     message = shape((16, halo_width), F32)
     vector_shape = shape((probes, rows_dev), F32)
+    source_shape = shape((row_blocks + 1, 16, edge), BF16)
     to_low, to_up, vector, scale, source = call(
         first_kernel,
-        [SMEM, SMEM, SMEM, SMEM, ANY] + [VMEM] * (4 + groups),
-        (message, message, vector_shape, vector_shape, shape(source_shape, BF16)),
+        [SMEM, SMEM] + [VMEM] * (6 + groups),
+        (message, message, vector_shape, vector_shape, source_shape),
         (VMEM,) * 5,
-        [tile_scratch, table, spread, sums, sems],
+        [spread, sums],
         "first",
-    )(counts, halo, sizes, place, blocks, boundary, degree, got_low, got_up, *starts)
+    )(halo, sizes, blocks, boundary, table, degree, got_low, got_up, *starts)
 
     vectors = [vector]
     for step in range(STEPS):
         got_low, got_up = exchange(to_low, to_up)
         image = call(
             own_kernel,
-            [SMEM, SMEM, SMEM, ANY, VMEM],
+            [SMEM, SMEM, VMEM, VMEM],
             vector_shape,
             VMEM,
-            [tile_scratch, sums, sems],
+            [sums],
             f"own{step}",
-        )(counts, own, sizes, blocks, source)
-        scratch = [
-            tile_scratch, table, spread, sums, pltpu.VMEM((2 * halo_blocks + 1, 16, edge), BF16), sems,
-        ]
+        )(own, sizes, blocks, source)
         if step + 1 < STEPS:
             to_low, to_up, vector, source = call(
                 functools.partial(middle_kernel, SHIFTS[step]),
-                [SMEM, SMEM, SMEM, ANY] + [VMEM] * 6,
-                (message, message, vector_shape, shape(source_shape, BF16)),
+                [SMEM, SMEM] + [VMEM] * 8,
+                (message, message, vector_shape, source_shape),
                 (VMEM,) * 4,
-                scratch,
+                [spread, sums, outside],
                 f"middle{step}",
-            )(counts, halo, sizes, blocks, boundary, vectors[-1], scale, image, got_low, got_up)
+            )(halo, sizes, blocks, boundary, table, vectors[-1], scale, image, got_low, got_up)
         else:
             grams, vector = call(
                 functools.partial(last_kernel, SHIFTS[step]),
-                [SMEM, SMEM, SMEM, ANY] + [VMEM] * (5 + STEPS),
+                [SMEM, SMEM] + [VMEM] * (7 + STEPS),
                 (shape((8 * parts, 128), F32), vector_shape),
                 (VMEM,) * 2,
-                scratch,
+                [spread, sums, outside],
                 "last",
-            )(counts, halo, sizes, blocks, boundary, scale, image, got_low, got_up, *vectors)
+            )(halo, sizes, blocks, boundary, table, scale, image, got_low, got_up, *vectors)
         vectors.append(vector)
     gathered = lax.all_to_all(grams, "rows", 0, 0, tiled=True)
     return call(
         functools.partial(final_kernel, float(node_total)),
-        [SMEM] + [VMEM] * (2 + STEPS),
+        [VMEM] * (2 + STEPS),
         (
             shape((each, rows_dev), F32),
             shape((STEPS, probes, probes), F32),
@@ -525,7 +505,7 @@
         (VMEM,) * 3,
         [],
         "final",
-    )(place, gathered, *vectors)
+    )(gathered, *vectors)
 
 
 def solution(mesh):

time: 84.8 us -> 77.1 us (0.909)
  starting transfers between devices: 33.5 us -> 22.7 us
  waiting for transfers between devices: 4.54 us -> 13.9 us
  local copies, waits for them, and re-layouts: 5.69 us -> 1.32 us
  blocking collectives: 14.5 us -> 12 us
    ppermute x4, starting transfers between devices: 28 us -> 3.77 us  [exchange(): from_up = lax.ppermute(to_low, 'rows', backward)]
    ppermute x4, starting transfers between devices: 2.21 us -> 15.6 us  [exchange(): from_low = lax.ppermute(to_up, 'rows', forward)]
    ppermute x4, waiting for transfers between devices: 0.01 us -> 4.86 us  [exchange(): from_up = lax.ppermute(to_low, 'rows', backward)]
    ppermute x4, waiting for transfers between devices: 4.52 us -> 9.02 us  [exchange(): from_low = lax.ppermute(to_up, 'rows', forward)]
    unnamed x12 -> x10, local copies, waits for them, and re-layouts: 5.69 us -> 1.32 us
    all_to_all x1, blocking collectives: 14.5 us -> 12 us  [local(): gathered = lax.all_to_all(grams, 'rows', 0, 0, tiled=True)]
    pallas_call x10 -> x11, Pallas kernels: 24.1 us -> 24.5 us  [the longest x2 6.91 us: local(): call(functools.partial(middle_kernel, SHIFTS[step]), [SMEM, SMEM] + [VMEM...]
  transfers between devices with their start and end apart: 11 -> 11, of which waited for: 3 -> 6; matrix products, arithmetic and copies ran while one was open for 0% -> 0% of each run, Pallas kernels for 10% -> 11%
where the time goes in v1:
time: 77.1 us; the launch traced here: 75.8 us
  Pallas kernels  24.5 us (32%)
  starting transfers between devices  22.7 us (29%)
  waiting for transfers between devices  13.9 us (18%)
  blocking collectives  12 us (16%)
  between operations  1.45 us (2%)
  local copies, waits for them, and re-layouts  1.32 us (2%)
    ppermute x4, starting transfers between devices, exchange(): from_low = lax.ppermute(to_up, 'rows', forward)  15.6 us
    all_to_all x1, blocking collectives, local(): gathered = lax.all_to_all(grams, 'rows', 0, 0, tiled=True)  12 us
    ppermute x4, waiting for transfers between devices, exchange(): from_low = lax.ppermute(to_up, 'rows', forward)  9.02 us
    pallas_call x2, Pallas kernels, local(): call(functools.partial(middle_kernel, SHIFTS[step]), [SMEM, SMEM] + [VMEM...  6.91 us
    ppermute x4, waiting for transfers between devices, exchange(): from_up = lax.ppermute(to_low, 'rows', backward)  4.86 us
    pallas_call x1, Pallas kernels, local(): call(functools.partial(final_kernel, float(node_total)), [VMEM] * (2 + ST...  4.06 us
    ppermute x4, starting transfers between devices, exchange(): from_up = lax.ppermute(to_low, 'rows', backward)  3.77 us
    pallas_call x3, Pallas kernels, local(): call(own_kernel, [SMEM, SMEM, VMEM, VMEM], vector_shape, VMEM, [sums], f'...  3.67 us
  transfers between devices with their start and end apart: 11, of which 6 were waited for; matrix products, arithmetic and copies ran while one was open for 0% of the time, Pallas kernels for 11%

profile of v1, /device:TPU:0, one launch (start us, length us, event | category | flops | bytes accessed | tf_op | source)
XLA Modules:
  0.0 75.8 jit_solution(5989701079773643730)
XLA Ops:
  0.6 0.0 copy-start
  0.6 3.1 %collective-permute-start.3 = (f32[2,4096]{1,0:T(2,128)}, f32[2,4096]{1,0:T(2,128)S(1)}, u32[]{:S(2)}, u32[]{:S(2)}) collective-permute-start(f32[2,4096]{1,0:T(2,128)} %rest_0_.1), channel_id=1, source_target_pairs={{0,2},{1,3},{2,0},{3,1},{4,6},{5,7},{6,4},{7,5},{8,10},{9,11},{10,... | collective-permute-start | bytes 98312 | tf_op jit(solution)/shard_map/ppermute | solution.py:420
  3.7 0.0 collective-permute-start.2
  3.7 0.2 collective-permute-start.4
  4.5 0.0 copy-start.3
  4.6 0.6 copy-done.3
  5.2 0.0 copy-start.4
  5.2 0.7 copy-done.4
  5.9 1.6 %lists.1 = (s32[136]{0:T(256)S(1)}, s32[136]{0:T(256)S(1)}, s32[2]{0:T(128)S(1)}) custom-call(s32[1]{0:T(128)S(6)} %copy.9.counts_in, s32[128]{0:T(128)S(1)} %copy-done.3, s32[128]{0:T(128)S(1)} %copy-done.4), custom_call_target="tpu_custom_call" | custom-call | flops 2147483648 | bytes 1048576 | tf_op jit(solution)/shard_map/lists/pallas_call | solution.py:423
  7.5 0.0 copy-start.2
  7.5 0.0 copy-done
  7.5 0.8 %setup.1 = (f32[16,128]{1,0:T(8,128)S(1)}, f32[16,128]{1,0:T(8,128)S(1)}) custom-call(s32[136]{0:T(256)S(1)} %get-tuple-element.25.halo, s32[2]{0:T(128)S(1)} %get-tuple-element.26.sizes, bf16[128,128,128]{2,1,0:T(8,128)(2,1)S(1)} %copy-done), custom_call_target="tpu_custom_call" | custom-call | flops 2147483648 | bytes 1048576 | tf_op jit(solution)/shard_map/setup/pallas_call | solution.py:436
  8.2 0.0 copy-start.1
  8.3 3.4 %collective-permute-start = (f32[16,128]{1,0:T(8,128)S(1)}, f32[16,128]{1,0:T(8,128)S(1)}, u32[]{:S(2)}, u32[]{:S(2)}) collective-permute-start(f32[16,128]{1,0:T(8,128)S(1)} %get-tuple-element.30), channel_id=1, source_target_pairs={{0,4},{4,8},{8,12},{12,16},{16,20},{20,24},{24,28},{28,0},{1,5},{5... | collective-permute-start | bytes 24584 | tf_op jit(solution)/shard_map/ppermute | solution.py:398
  11.6 1.7 %collective-permute-start.1 = (f32[16,128]{1,0:T(8,128)S(1)}, f32[16,128]{1,0:T(8,128)S(1)}, u32[]{:S(2)}, u32[]{:S(2)}) collective-permute-start(f32[16,128]{1,0:T(8,128)S(1)} %get-tuple-element.31), channel_id=1, source_target_pairs={{4,0},{8,4},{12,8},{16,12},{20,16},{24,20},{28,24},{0,28},{5,1},{9... | collective-permute-start | bytes 24584 | tf_op jit(solution)/shard_map/ppermute | solution.py:397
  13.3 0.0 copy-done.2
  13.3 2.2 %degree.1 = (f32[8,4096]{1,0:T(8,128)S(1)}, bf16[256,4096]{1,0:T(8,128)(2,1)S(1)}) custom-call(s32[136]{0:T(256)S(1)} %get-tuple-element.27.own, s32[136]{0:T(256)S(1)} %get-tuple-element.25.halo, s32[2]{0:T(128)S(1)} %get-tuple-element.26.sizes, bf16[128,128,128]{2,1,0:T(8,128)(2,1)S(1)} %copy-done, s32[2,2048]{1,0:T(2,128)S(1)} %copy-done.2), custom_call_target="tpu_custom_call" | custom-call | flops 2147483648 | bytes 1048576 | tf_op jit(solution)/shard_map/degree/pallas_call | solution.py:445
  15.6 0.0 collective-permute-done.got_low
  15.6 0.0 collective-permute-done.1.got_up
  15.6 0.0 collective-permute-done.3.rest_2_
  15.6 0.0 collective-permute-done.2.rest_1_
  15.6 0.0 collective-permute-done.4.rest_3_
  15.6 0.0 copy-done.1
  15.6 2.6 %first.1 = (f32[16,2048]{1,0:T(8,128)S(1)}, f32[16,2048]{1,0:T(8,128)S(1)}, f32[8,4096]{1,0:T(8,128)S(1)}, f32[8,4096]{1,0:T(8,128)S(1)}, bf16[33,16,128]{2,1,0:T(8,128)(2,1)S(1)}) custom-call(s32[136]{0:T(256)S(1)} %get-tuple-element.25.halo, s32[2]{0:T(128)S(1)} %get-tuple-element.26.sizes, bf16[128,128,128]{2,1,0:T(8,128)(2,1)S(1)} %copy-done, ...), custom_call_target="tpu_custom_call" | custom-call | flops 2147483648 | bytes 1048576 | tf_op jit(solution)/shard_map/first/pallas_call | solution.py:457
  18.3 4.6 %collective-permute-start.5 = (f32[16,2048]{1,0:T(8,128)S(1)}, f32[16,2048]{1,0:T(8,128)S(1)}, u32[]{:S(2)}, u32[]{:S(2)}) collective-permute-start(f32[16,2048]{1,0:T(8,128)S(1)} %get-tuple-element.35), channel_id=1, source_target_pairs={{0,4},{4,8},{8,12},{12,16},{16,20},{20,24},{24,28},{28,0},{1,5},{5... | collective-permute-start | bytes 393224 | tf_op jit(solution)/shard_map/ppermute | solution.py:398
  22.8 0.2 collective-permute-start.6
  23.1 1.2 %own0.1.image = f32[8,4096]{1,0:T(8,128)S(1)} custom-call(s32[136]{0:T(256)S(1)} %get-tuple-element.27.own, s32[2]{0:T(128)S(1)} %get-tuple-element.26.sizes, bf16[128,128,128]{2,1,0:T(8,128)(2,1)S(1)} %copy-done, bf16[33,16,128]{2,1,0:T(8,128)(2,1)S(1)} %get-tuple-element.34.source), custom_call_target="tpu_custom_call" | custom-call | flops 2147483648 | bytes 1048576 | tf_op jit(solution)/shard_map/own0/pallas_call | solution.py:469
  24.3 3.7 %collective-permute-done.5.got_low = f32[16,2048]{1,0:T(8,128)S(1)} collective-permute-done((f32[16,2048]{1,0:T(8,128)S(1)}, f32[16,2048]{1,0:T(8,128)S(1)}, u32[]{:S(2)}, u32[]{:S(2)}) %collective-permute-start.5) | collective-permute-done | bytes 131104 | tf_op jit(solution)/shard_map/ppermute | solution.py:398
  28.0 0.9 %collective-permute-done.6.got_up = f32[16,2048]{1,0:T(8,128)S(1)} collective-permute-done((f32[16,2048]{1,0:T(8,128)S(1)}, f32[16,2048]{1,0:T(8,128)S(1)}, u32[]{:S(2)}, u32[]{:S(2)}) %collective-permute-start.6) | collective-permute-done | bytes 131104 | tf_op jit(solution)/shard_map/ppermute | solution.py:397
  29.0 3.5 %middle0.1 = (f32[16,2048]{1,0:T(8,128)S(1)}, f32[16,2048]{1,0:T(8,128)S(1)}, f32[8,4096]{1,0:T(8,128)S(1)}, bf16[33,16,128]{2,1,0:T(8,128)(2,1)S(1)}) custom-call(s32[136]{0:T(256)S(1)} %get-tuple-element.25.halo, s32[2]{0:T(128)S(1)} %get-tuple-element.26.sizes, bf16[128,128,128]{2,1,0:T(8,128)(2,1)S(1)} %copy-done, s32[2,2048]{1,0:T(2,128)S(1)} %copy-done.2, ...), custom_call_target="tpu_custom_call" | custom-call | flops 2147483648 | bytes 1048576 | tf_op jit(solution)/shard_map/middle0/pallas_call | solution.py:478
  32.4 4.3 %collective-permute-start.7 = (f32[16,2048]{1,0:T(8,128)S(1)}, f32[16,2048]{1,0:T(8,128)S(1)}, u32[]{:S(2)}, u32[]{:S(2)}) collective-permute-start(f32[16,2048]{1,0:T(8,128)S(1)} %get-tuple-element.39), channel_id=1, source_target_pairs={{0,4},{4,8},{8,12},{12,16},{16,20},{20,24},{24,28},{28,0},{1,5},{5... | collective-permute-start | bytes 393224 | tf_op jit(solution)/shard_map/ppermute | solution.py:398
  36.7 0.5 collective-permute-start.8
  37.2 1.2 %own1.1.image = f32[8,4096]{1,0:T(8,128)S(1)} custom-call(s32[136]{0:T(256)S(1)} %get-tuple-element.27.own, s32[2]{0:T(128)S(1)} %get-tuple-element.26.sizes, bf16[128,128,128]{2,1,0:T(8,128)(2,1)S(1)} %copy-done, bf16[33,16,128]{2,1,0:T(8,128)(2,1)S(1)} %get-tuple-element.38.source), custom_call_target="tpu_custom_call" | custom-call | flops 2147483648 | bytes 1048576 | tf_op jit(solution)/shard_map/own1/pallas_call | solution.py:469
  38.4 3.0 %collective-permute-done.7.got_low = f32[16,2048]{1,0:T(8,128)S(1)} collective-permute-done((f32[16,2048]{1,0:T(8,128)S(1)}, f32[16,2048]{1,0:T(8,128)S(1)}, u32[]{:S(2)}, u32[]{:S(2)}) %collective-permute-start.7) | collective-permute-done | bytes 131104 | tf_op jit(solution)/shard_map/ppermute | solution.py:398
  41.5 1.8 %collective-permute-done.8.got_up = f32[16,2048]{1,0:T(8,128)S(1)} collective-permute-done((f32[16,2048]{1,0:T(8,128)S(1)}, f32[16,2048]{1,0:T(8,128)S(1)}, u32[]{:S(2)}, u32[]{:S(2)}) %collective-permute-start.8) | collective-permute-done | bytes 131104 | tf_op jit(solution)/shard_map/ppermute | solution.py:397
  43.2 3.5 %middle1.1 = (f32[16,2048]{1,0:T(8,128)S(1)}, f32[16,2048]{1,0:T(8,128)S(1)}, f32[8,4096]{1,0:T(8,128)S(1)}, bf16[33,16,128]{2,1,0:T(8,128)(2,1)S(1)}) custom-call(s32[136]{0:T(256)S(1)} %get-tuple-element.25.halo, s32[2]{0:T(128)S(1)} %get-tuple-element.26.sizes, bf16[128,128,128]{2,1,0:T(8,128)(2,1)S(1)} %copy-done, s32[2,2048]{1,0:T(2,128)S(1)} %copy-done.2, ...), custom_call_target="tpu_custom_call" | custom-call | flops 2147483648 | bytes 1048576 | tf_op jit(solution)/shard_map/middle1/pallas_call | solution.py:478
  46.7 3.4 %collective-permute-start.9 = (f32[16,2048]{1,0:T(8,128)S(1)}, f32[16,2048]{1,0:T(8,128)S(1)}, u32[]{:S(2)}, u32[]{:S(2)}) collective-permute-start(f32[16,2048]{1,0:T(8,128)S(1)} %get-tuple-element.42), channel_id=1, source_target_pairs={{0,4},{4,8},{8,12},{12,16},{16,20},{20,24},{24,28},{28,0},{1,5},{5... | collective-permute-start | bytes 393224 | tf_op jit(solution)/shard_map/ppermute | solution.py:398
  50.1 1.4 %collective-permute-start.10 = (f32[16,2048]{1,0:T(8,128)S(1)}, f32[16,2048]{1,0:T(8,128)S(1)}, u32[]{:S(2)}, u32[]{:S(2)}) collective-permute-start(f32[16,2048]{1,0:T(8,128)S(1)} %get-tuple-element.43), channel_id=1, source_target_pairs={{4,0},{8,4},{12,8},{16,12},{20,16},{24,20},{28,24},{0,28},{5,1},{9... | collective-permute-start | bytes 393224 | tf_op jit(solution)/shard_map/ppermute | solution.py:397
  51.5 1.2 %own2.1.image = f32[8,4096]{1,0:T(8,128)S(1)} custom-call(s32[136]{0:T(256)S(1)} %get-tuple-element.27.own, s32[2]{0:T(128)S(1)} %get-tuple-element.26.sizes, bf16[128,128,128]{2,1,0:T(8,128)(2,1)S(1)} %copy-done, bf16[33,16,128]{2,1,0:T(8,128)(2,1)S(1)} %get-tuple-element.41.source), custom_call_target="tpu_custom_call" | custom-call | flops 2147483648 | bytes 1048576 | tf_op jit(solution)/shard_map/own2/pallas_call | solution.py:469
  52.7 2.3 %collective-permute-done.9.got_low = f32[16,2048]{1,0:T(8,128)S(1)} collective-permute-done((f32[16,2048]{1,0:T(8,128)S(1)}, f32[16,2048]{1,0:T(8,128)S(1)}, u32[]{:S(2)}, u32[]{:S(2)}) %collective-permute-start.9) | collective-permute-done | bytes 131104 | tf_op jit(solution)/shard_map/ppermute | solution.py:398
  55.0 2.1 %collective-permute-done.10.got_up = f32[16,2048]{1,0:T(8,128)S(1)} collective-permute-done((f32[16,2048]{1,0:T(8,128)S(1)}, f32[16,2048]{1,0:T(8,128)S(1)}, u32[]{:S(2)}, u32[]{:S(2)}) %collective-permute-start.10) | collective-permute-done | bytes 131104 | tf_op jit(solution)/shard_map/ppermute | solution.py:397
  57.1 2.6 %last.1 = (f32[64,128]{1,0:T(8,128)S(1)}, f32[8,4096]{1,0:T(8,128)S(1)}) custom-call(s32[136]{0:T(256)S(1)} %get-tuple-element.25.halo, s32[2]{0:T(128)S(1)} %get-tuple-element.26.sizes, bf16[128,128,128]{2,1,0:T(8,128)(2,1)S(1)} %copy-done, s32[2,2048]{1,0:T(2,128)S(1)} %copy-done.2, bf16[256,4096]{1,0:T(8,128)(2,1)S(1)} %get-tuple-element.28.table, ...), custom_call_target="tpu_custom_call" | custom-call | flops 2147483648 | bytes 1048576 | tf_op jit(solution)/shard_map/last/pallas_call | solution.py:487
  59.7 12.0 %all_to_all.11 = f32[8,8,128]{2,1,0:T(8,128)S(1)} all-to-all(f32[8,8,128]{2,1,0:T(8,128)S(1)} %bitcast.2), channel_id=1, replica_groups=mesh['rows'=8,'probe'=4] {'rows'}, dimensions={0} | all-to-all | bytes 65536 | tf_op jit(solution)/shard_map/all_to_all | solution.py:496
  71.7 4.1 %final.1 = (f32[2,4096]{1,0:T(2,128)}, f32[3,8,8]{2,1,0:T(8,128)}, f32[3,8,8]{2,1,0:T(8,128)}) custom-call(f32[64,128]{1,0:T(8,128)S(1)} %bitcast.3, f32[8,4096]{1,0:T(8,128)S(1)} %get-tuple-element.33.previous.rest_0_, f32[8,4096]{1,0:T(8,128)S(1)} %get-tuple-element.37.previous.rest_1_, f32[8,4096]{1,0:T(8,128)S(1)} %get-tuple-element.44.rest_2_, ...), custom_call_target="tpu_custom_call" | custom-call | flops 2147483648 | bytes 1048576 | tf_op jit(solution)/shard_map/final/pallas_call | solution.py:497
Async XLA Ops:
  0.6 6.8 %copy-start = (bf16[128,128,128]{2,1,0:T(8,128)(2,1)S(1)}, bf16[128,128,128]{2,1,0:T(8,128)(2,1)}, u32[]{:S(2)}) copy-start(bf16[128,128,128]{2,1,0:T(8,128)(2,1)} %tiles.17) | copy-start | bytes 12582916
  0.6 15.0 %collective-permute-start.3 = (f32[2,4096]{1,0:T(2,128)}, f32[2,4096]{1,0:T(2,128)S(1)}, u32[]{:S(2)}, u32[]{:S(2)}) collective-permute-start(f32[2,4096]{1,0:T(2,128)} %rest_0_.1), channel_id=1, source_target_pairs={{0,2},{1,3},{2,0},{3,1},{4,6},{5,7},{6,4},{7,5},{8,10},{9,11},{10,... | collective-permute-start | bytes 98312 | tf_op jit(solution)/shard_map/ppermute | solution.py:420
  3.7 11.9 %collective-permute-start.2 = (f32[2,4096]{1,0:T(2,128)}, f32[2,4096]{1,0:T(2,128)S(1)}, u32[]{:S(2)}, u32[]{:S(2)}) collective-permute-start(f32[2,4096]{1,0:T(2,128)} %rest_0_.1), channel_id=1, source_target_pairs={{0,1},{1,0},{2,3},{3,2},{4,5},{5,4},{6,7},{7,6},{8,9},{9,8},{10,11... | collective-permute-start | bytes 98312 | tf_op jit(solution)/shard_map/ppermute | solution.py:420
  3.7 11.9 %collective-permute-start.4 = (f32[2,4096]{1,0:T(2,128)}, f32[2,4096]{1,0:T(2,128)S(1)}, u32[]{:S(2)}, u32[]{:S(2)}) collective-permute-start(f32[2,4096]{1,0:T(2,128)} %rest_0_.1), channel_id=1, source_target_pairs={{0,3},{1,2},{2,1},{3,0},{4,7},{5,6},{6,5},{7,4},{8,11},{9,10},{10,... | collective-permute-start | bytes 98312 | tf_op jit(solution)/shard_map/ppermute | solution.py:420
  4.5 0.7 copy-start.3
  5.2 0.7 copy-start.4
  7.5 5.9 %copy-start.2 = (s32[2,2048]{1,0:T(2,128)S(1)}, s32[2,2048]{1,0:T(2,128)}, u32[]{:S(2)}) copy-start(s32[2,2048]{1,0:T(2,128)} %bound.9) | copy-start | bytes 49156
  8.2 7.4 %copy-start.1 = (f32[2,4096]{1,0:T(2,128)S(1)}, f32[2,4096]{1,0:T(2,128)}, u32[]{:S(2)}) copy-start(f32[2,4096]{1,0:T(2,128)} %rest_0_.1) | copy-start | bytes 98308
  8.3 7.3 %collective-permute-start = (f32[16,128]{1,0:T(8,128)S(1)}, f32[16,128]{1,0:T(8,128)S(1)}, u32[]{:S(2)}, u32[]{:S(2)}) collective-permute-start(f32[16,128]{1,0:T(8,128)S(1)} %get-tuple-element.30), channel_id=1, source_target_pairs={{0,4},{4,8},{8,12},{12,16},{16,20},{20,24},{24,28},{28,0},{1,5},{5... | collective-permute-start | bytes 24584 | tf_op jit(solution)/shard_map/ppermute | solution.py:398
  11.6 4.0 %collective-permute-start.1 = (f32[16,128]{1,0:T(8,128)S(1)}, f32[16,128]{1,0:T(8,128)S(1)}, u32[]{:S(2)}, u32[]{:S(2)}) collective-permute-start(f32[16,128]{1,0:T(8,128)S(1)} %get-tuple-element.31), channel_id=1, source_target_pairs={{4,0},{8,4},{12,8},{16,12},{20,16},{24,20},{28,24},{0,28},{5,1},{9... | collective-permute-start | bytes 24584 | tf_op jit(solution)/shard_map/ppermute | solution.py:397
  18.3 9.7 %collective-permute-start.5 = (f32[16,2048]{1,0:T(8,128)S(1)}, f32[16,2048]{1,0:T(8,128)S(1)}, u32[]{:S(2)}, u32[]{:S(2)}) collective-permute-start(f32[16,2048]{1,0:T(8,128)S(1)} %get-tuple-element.35), channel_id=1, source_target_pairs={{0,4},{4,8},{8,12},{12,16},{16,20},{20,24},{24,28},{28,0},{1,5},{5... | collective-permute-start | bytes 393224 | tf_op jit(solution)/shard_map/ppermute | solution.py:398
  22.8 6.1 %collective-permute-start.6 = (f32[16,2048]{1,0:T(8,128)S(1)}, f32[16,2048]{1,0:T(8,128)S(1)}, u32[]{:S(2)}, u32[]{:S(2)}) collective-permute-start(f32[16,2048]{1,0:T(8,128)S(1)} %get-tuple-element.36), channel_id=1, source_target_pairs={{4,0},{8,4},{12,8},{16,12},{20,16},{24,20},{28,24},{0,28},{5,1},{9... | collective-permute-start | bytes 393224 | tf_op jit(solution)/shard_map/ppermute | solution.py:397
  32.4 9.0 %collective-permute-start.7 = (f32[16,2048]{1,0:T(8,128)S(1)}, f32[16,2048]{1,0:T(8,128)S(1)}, u32[]{:S(2)}, u32[]{:S(2)}) collective-permute-start(f32[16,2048]{1,0:T(8,128)S(1)} %get-tuple-element.39), channel_id=1, source_target_pairs={{0,4},{4,8},{8,12},{12,16},{16,20},{20,24},{24,28},{28,0},{1,5},{5... | collective-permute-start | bytes 393224 | tf_op jit(solution)/shard_map/ppermute | solution.py:398
  36.7 6.6 %collective-permute-start.8 = (f32[16,2048]{1,0:T(8,128)S(1)}, f32[16,2048]{1,0:T(8,128)S(1)}, u32[]{:S(2)}, u32[]{:S(2)}) collective-permute-start(f32[16,2048]{1,0:T(8,128)S(1)} %get-tuple-element.40), channel_id=1, source_target_pairs={{4,0},{8,4},{12,8},{16,12},{20,16},{24,20},{28,24},{0,28},{5,1},{9... | collective-permute-start | bytes 393224 | tf_op jit(solution)/shard_map/ppermute | solution.py:397
  46.7 8.3 %collective-permute-start.9 = (f32[16,2048]{1,0:T(8,128)S(1)}, f32[16,2048]{1,0:T(8,128)S(1)}, u32[]{:S(2)}, u32[]{:S(2)}) collective-permute-start(f32[16,2048]{1,0:T(8,128)S(1)} %get-tuple-element.42), channel_id=1, source_target_pairs={{0,4},{4,8},{8,12},{12,16},{16,20},{20,24},{24,28},{28,0},{1,5},{5... | collective-permute-start | bytes 393224 | tf_op jit(solution)/shard_map/ppermute | solution.py:398
  50.1 7.0 %collective-permute-start.10 = (f32[16,2048]{1,0:T(8,128)S(1)}, f32[16,2048]{1,0:T(8,128)S(1)}, u32[]{:S(2)}, u32[]{:S(2)}) collective-permute-start(f32[16,2048]{1,0:T(8,128)S(1)} %get-tuple-element.43), channel_id=1, source_target_pairs={{4,0},{8,4},{12,8},{16,12},{20,16},{24,20},{28,24},{0,28},{5,1},{9... | collective-permute-start | bytes 393224 | tf_op jit(solution)/shard_map/ppermute | solution.py:397
